TPU v7x, 32 devices: a whole 2x2x4 slice. The times are simulated.
32 devices in a mesh: dp: 8 (over y, x, core), tensor: 4 (over z).
Axes of the slice: x: 2, y: 2, z: 4, core: 2. Of those that a mesh axis runs over, the one named last changes fastest.
Arguments:
- hidden_in: bfloat16 [1024, 2048], P('dp'), may hold values from -6 to 6
- attn_gain: float32 [2048], replicated, may hold values from 0.5 to 1.5
- query_weight: bfloat16 [2048, 2048], P('dp', 'tensor'), may hold values from -0.125 to 0.125
- key_weight: bfloat16 [2048, 2048], P('dp', 'tensor'), may hold values from -0.125 to 0.125
- value_weight: bfloat16 [2048, 2048], P('dp', 'tensor'), may hold values from -0.125 to 0.125
- output_weight: bfloat16 [2048, 2048], P('dp', 'tensor'), may hold values from -1.5 to 1.5
- query_gain: float32 [2048], P('tensor'), may hold values from 0.5 to 1.5
- key_gain: float32 [2048], P('tensor'), may hold values from 0.5 to 1.5
- moe_gain: float32 [2048], replicated, may hold values from 0.5 to 1.5
- expert_gate_up: bfloat16 [2048, 16, 2, 1024], P(None, 'dp', None, 'tensor'), may hold values from -0.125 to 0.125
- expert_down: bfloat16 [2048, 16, 1024], P(None, 'dp', 'tensor'), may hold values from -0.1875 to 0.1875
- experts: int32 [1024, 8], P('dp'), may hold values from 0 to 15, all different within a row
- gates: float32 [1024, 8], P('dp'), may hold values from 0.25 to 0.75
- anchor: int32 [1024], P('dp'), may hold values from 0 to 1023, each once
- lengths: int32 [4], replicated, may hold values from 1 to 512, 1024 in all
- cotangent: bfloat16 [1024, 2048], P('dp'), may hold values from -8 to 8
Outputs:
- output: bfloat16 [1024, 2048], P('dp')
- input_grad: float32 [1024, 2048], P('dp')
- query_grad: float32 [2048, 2048], P('dp', 'tensor')
- key_grad: float32 [2048, 2048], P('dp', 'tensor')
- value_grad: float32 [2048, 2048], P('dp', 'tensor')
- output_grad: float32 [2048, 2048], P('dp', 'tensor')
- gate_up_grad: float32 [2048, 16, 2, 1024], P(None, 'dp', None, 'tensor')
- down_grad: float32 [2048, 16, 1024], P(None, 'dp', 'tensor')
- attn_gain_grad: float32 [2048], P('dp')
- query_gain_grad: float32 [2048], P('dp')
- key_gain_grad: float32 [2048], P('dp')
- moe_gain_grad: float32 [2048], P('dp')
Inputs may be any that keep to these rules, and one draw needn't show every extreme that they name: `anchor`: each number appears once. The lengths sum to 1024; the longest is exactly 512. Each row names 8 different experts.
All inputs are finite; a program needn't handle non-finite values.
Results may differ from a plain program's by a relative error of at most 0.033.
Values may be sent and summed in bfloat16 or wider, within the bound.
A program may use at most 256 MiB of HBM per device.

v0:
```python
import jax
import jax.numpy as jnp
from jax import lax
from jax.sharding import PartitionSpec as P

D = 2048
HD = 128
TOPK = 8
EPSILON = 1e-05
ROPE_BASE = 10000.0
NEG_FILL = -1e30


def rms_norm(values, gain):
    return values * lax.rsqrt(jnp.mean(values * values, axis=-1, keepdims=True) + EPSILON) * gain


def norm_back(values, gain, grad_out):
    inv_rms = lax.rsqrt(jnp.mean(values * values, axis=-1, keepdims=True) + EPSILON)
    weighted = grad_out * gain
    grad_in = inv_rms * weighted - values * inv_rms**3 * jnp.mean(
        weighted * values, axis=-1, keepdims=True
    )
    return (grad_in, jnp.sum(grad_out * values * inv_rms, axis=0))


def locate(anchor, lengths):
    ends = jnp.cumsum(lengths)
    starts = ends - lengths
    docs = jnp.sum((anchor[:, None] >= ends[None, :]).astype(jnp.int32), axis=1)
    which = docs[:, None] == jnp.arange(lengths.shape[0], dtype=jnp.int32)[None, :]
    begins = jnp.sum(jnp.where(which, starts[None, :], 0), axis=1)
    return (docs, (anchor - begins).astype(jnp.int32))


def rotary(tensor, positions):
    half_dim = HD // 2
    freqs = ROPE_BASE ** (-2.0 * jnp.arange(half_dim, dtype=jnp.float32) / HD)
    angles = positions.astype(jnp.float32)[:, None] * freqs[None, :]
    cosine = jnp.cos(angles)[:, None, :]
    sine_part = jnp.sin(angles)[:, None, :]
    first_half = tensor[..., :half_dim]
    second_half = tensor[..., half_dim:]
    return jnp.concatenate(
        [
            first_half * cosine - second_half * sine_part,
            second_half * cosine + first_half * sine_part,
        ],
        axis=-1,
    )


def routing(expert_rows, gate_rows, num_exp, capacity):
    tok_count = expert_rows.shape[0]
    flat_ids = expert_rows.reshape(-1)
    one_hot = (flat_ids[:, None] == jnp.arange(num_exp, dtype=jnp.int32)[None, :]).astype(jnp.int32)
    earlier = jnp.cumsum(one_hot, axis=0) - one_hot
    slot_ids = jnp.sum(earlier * one_hot, axis=1)
    dest_rows = jnp.where(slot_ids < capacity, flat_ids * capacity + slot_ids, num_exp * capacity)
    pair_token = jnp.arange(tok_count * TOPK, dtype=jnp.int32) // TOPK
    slot_source = jnp.zeros((num_exp * capacity + 1,), jnp.int32).at[dest_rows].set(pair_token)
    slot_filled = jnp.zeros((num_exp * capacity + 1,), jnp.float32).at[dest_rows].set(1.0)
    slot_gate = (
        jnp.zeros((num_exp * capacity + 1,), jnp.float32).at[dest_rows].set(gate_rows.reshape(-1))
    )
    return (dest_rows, slot_source[:-1], slot_filled[:-1], slot_gate[:-1])


def pair_allowed(query_anchor, query_docs, key_anchor, key_docs):
    return (
        (query_docs[:, None] == key_docs[None, :]) & (key_anchor[None, :] <= query_anchor[:, None])
    )[None]


def contract_last(left, right):
    return lax.dot_general(
        left, right, (((1,), (1,)), ((), ())), preferred_element_type=jnp.float32
    )


def contract_first(left, right):
    return lax.dot_general(
        left, right, (((0,), (0,)), ((), ())), preferred_element_type=jnp.float32
    )


def shards(
    hidden_in,
    attn_gain,
    query_weight,
    key_weight,
    value_weight,
    output_weight,
    query_gain,
    key_gain,
    moe_gain,
    expert_gate_up,
    expert_down,
    experts,
    gates,
    anchor,
    lengths,
    cotangent,
):
    tok_rows = hidden_in.shape[0]
    head_local = query_weight.shape[1] // HD
    score_scale = HD ** (-0.5)
    f32 = jnp.float32
    bf16 = jnp.bfloat16
    n_dp = lax.axis_size("dp")
    exp_local = expert_down.shape[1]
    num_exp = exp_local * n_dp
    capacity = 9 * tok_rows * TOPK // (8 * num_exp)
    inputs = hidden_in.astype(f32)
    grad_out = cotangent.astype(f32)
    docs, positions = locate(anchor, lengths)
    normed = rms_norm(inputs, attn_gain).astype(bf16)
    query_full, key_full, value_full, output_full = (
        lax.all_gather(query_weight, "dp", axis=0, tiled=True),
        lax.all_gather(key_weight, "dp", axis=0, tiled=True),
        lax.all_gather(value_weight, "dp", axis=0, tiled=True),
        lax.all_gather(output_weight, "dp", axis=0, tiled=True),
    )
    query_raw = jnp.dot(normed, query_full, preferred_element_type=f32)
    key_raw = jnp.dot(normed, key_full, preferred_element_type=f32)
    value_raw = jnp.dot(normed, value_full, preferred_element_type=f32)
    squares = lax.psum(
        (jnp.sum(query_raw * query_raw, axis=1), jnp.sum(key_raw * key_raw, axis=1)), "tensor"
    )
    query_inv = lax.rsqrt(squares[0] / D + EPSILON)[:, None]
    key_inv = lax.rsqrt(squares[1] / D + EPSILON)[:, None]
    query_rows = rotary(
        (query_raw * query_inv * query_gain).reshape(tok_rows, head_local, HD), positions
    ).astype(bf16)
    key_rows = rotary(
        (key_raw * key_inv * key_gain).reshape(tok_rows, head_local, HD), positions
    ).astype(bf16)
    value_rows = value_raw.astype(bf16).reshape(tok_rows, head_local, HD)
    run_max = jnp.full((head_local, tok_rows), NEG_FILL, f32)
    run_acc = jnp.zeros((tok_rows, head_local, HD), f32)
    key_piece = lax.all_gather(key_rows, "dp", axis=0, tiled=True)
    value_piece = lax.all_gather(value_rows, "dp", axis=0, tiled=True)
    anchor_piece = lax.all_gather(anchor, "dp", axis=0, tiled=True)
    piece_docs, unused = locate(anchor_piece, lengths)
    allowed = pair_allowed(anchor, docs, anchor_piece, piece_docs)
    scores = score_scale * jnp.einsum(
        "qhd,khd->hqk", query_rows, key_piece, preferred_element_type=f32
    )
    new_max = jnp.maximum(run_max, jnp.max(jnp.where(allowed, scores, NEG_FILL), axis=2))
    factor = jnp.exp(run_max - new_max)
    attn_probs = jnp.where(allowed, jnp.exp(scores - new_max[:, :, None]), 0.0)
    new_sum = jnp.sum(attn_probs, axis=2)
    update = jnp.einsum(
        "hqk,khd->qhd", attn_probs.astype(bf16), value_piece, preferred_element_type=f32
    )
    run_max, run_sum, run_acc = (new_max, new_sum, run_acc * factor.T[:, :, None] + update)
    log_total = run_max + jnp.log(run_sum)
    attended = run_acc / run_sum.T[:, :, None]
    attended_low = attended.reshape(tok_rows, -1).astype(bf16)
    attn_sum = lax.psum(
        contract_last(attended_low, output_full).astype(jnp.bfloat16), "tensor"
    ).astype(jnp.float32)
    residual = inputs + attn_sum
    moe_in = rms_norm(residual, moe_gain).astype(bf16)
    dest_rows, slot_source, slot_filled, slot_gate = routing(experts, gates, num_exp, capacity)
    buffer_rows = (moe_in[slot_source] * slot_filled[:, None].astype(bf16)).reshape(
        num_exp, capacity, D
    )
    slot_grad = (
        (grad_out[slot_source] * (slot_gate * slot_filled)[:, None])
        .astype(bf16)
        .reshape(num_exp, capacity, D)
    )
    recv_rows, recv_grad = (
        lax.all_to_all(buffer_rows, "dp", split_axis=0, concat_axis=1, tiled=True),
        lax.all_to_all(slot_grad, "dp", split_axis=0, concat_axis=1, tiled=True),
    )
    gate_up = jnp.einsum("ecd,dezf->eczf", recv_rows, expert_gate_up, preferred_element_type=f32)
    gate_part = gate_up[:, :, 0]
    up_part = gate_up[:, :, 1]
    activated = (jax.nn.silu(gate_part) * up_part).astype(bf16)
    expert_out = jnp.einsum("ecf,def->ecd", activated, expert_down, preferred_element_type=f32)
    grad_down = jnp.einsum("ecd,ecf->def", recv_grad, activated, preferred_element_type=f32)
    grad_act = jnp.einsum("ecd,def->ecf", recv_grad, expert_down, preferred_element_type=f32)
    sigmoid_gate = jax.nn.sigmoid(gate_part)
    grad_gate = grad_act * up_part * sigmoid_gate * (1.0 + gate_part * (1.0 - sigmoid_gate))
    grad_up = grad_act * jax.nn.silu(gate_part)
    grad_gateup = jnp.stack([grad_gate, grad_up], axis=2).astype(bf16)
    grad_gateup_w = jnp.einsum("ecd,eczf->dezf", recv_rows, grad_gateup, preferred_element_type=f32)
    grad_buffer = jnp.einsum(
        "eczf,dezf->ecd", grad_gateup, expert_gate_up, preferred_element_type=f32
    )
    back_out, back_grad = (
        lax.all_to_all(
            expert_out.astype(jnp.bfloat16), "dp", split_axis=1, concat_axis=0, tiled=True
        ).astype(expert_out.dtype),
        lax.all_to_all(
            grad_buffer.astype(jnp.bfloat16), "dp", split_axis=1, concat_axis=0, tiled=True
        ).astype(grad_buffer.dtype),
    )
    width = back_out.shape[2]
    zero_row = jnp.zeros((1, width), f32)
    table_rows = jnp.concatenate([back_out.reshape(num_exp * capacity, width), zero_row], axis=0)
    combined = jnp.sum(
        table_rows[dest_rows].reshape(tok_rows, TOPK, width) * gates[:, :, None], axis=1
    )
    grad_table = jnp.concatenate([back_grad.reshape(num_exp * capacity, width), zero_row], axis=0)
    grad_moe_part = jnp.sum(grad_table[dest_rows].reshape(tok_rows, TOPK, width), axis=1)
    moe_sum, grad_moe_in = (
        lax.psum(combined.astype(jnp.bfloat16), "tensor").astype(jnp.float32),
        lax.psum(grad_moe_part.astype(jnp.bfloat16), "tensor").astype(jnp.float32),
    )
    output = (residual + moe_sum).astype(bf16)
    query_full, key_full, value_full, output_full = (
        lax.all_gather(query_weight, "dp", axis=0, tiled=True),
        lax.all_gather(key_weight, "dp", axis=0, tiled=True),
        lax.all_gather(value_weight, "dp", axis=0, tiled=True),
        lax.all_gather(output_weight, "dp", axis=0, tiled=True),
    )
    grad_norm_moe, grad_moe_gain = norm_back(residual, moe_gain, grad_moe_in)
    grad_resid = grad_out + grad_norm_moe
    grad_resid_low = grad_resid.astype(bf16)
    grad_output_w = contract_first(grad_resid_low, attended_low)
    grad_att_low = (
        jnp.dot(grad_resid_low, output_full, preferred_element_type=f32)
        .astype(bf16)
        .reshape(tok_rows, head_local, HD)
    )
    delta_rows = jnp.sum(grad_att_low.astype(f32) * attended, axis=2).T
    key_piece = lax.all_gather(key_rows, "dp", axis=0, tiled=True)
    value_piece = lax.all_gather(value_rows, "dp", axis=0, tiled=True)
    anchor_piece = lax.all_gather(anchor, "dp", axis=0, tiled=True)
    piece_docs, unused = locate(anchor_piece, lengths)
    allowed = pair_allowed(anchor, docs, anchor_piece, piece_docs)
    scores = score_scale * jnp.einsum(
        "qhd,khd->hqk", query_rows, key_piece, preferred_element_type=f32
    )
    attn_probs = jnp.where(allowed, jnp.exp(scores - log_total[:, :, None]), 0.0)
    grad_probs = jnp.einsum("qhd,khd->hqk", grad_att_low, value_piece, preferred_element_type=f32)
    grad_scores = (attn_probs * (grad_probs - delta_rows[:, :, None])).astype(bf16)
    grad_query_rot = score_scale * jnp.einsum(
        "hqk,khd->qhd", grad_scores, key_piece, preferred_element_type=f32
    )
    query_wide = lax.all_gather(
        query_rows.astype(f32).astype(jnp.bfloat16), "dp", axis=0, tiled=True
    ).astype(jnp.float32)
    gradatt_wide = lax.all_gather(
        grad_att_low.astype(f32).astype(jnp.bfloat16), "dp", axis=0, tiled=True
    ).astype(jnp.float32)
    logtot_piece = lax.all_gather(
        log_total.T.astype(jnp.bfloat16), "dp", axis=0, tiled=True
    ).astype(jnp.float32)
    delta_piece = lax.all_gather(
        delta_rows.T.astype(jnp.bfloat16), "dp", axis=0, tiled=True
    ).astype(jnp.float32)
    anchor_piece = lax.all_gather(anchor, "dp", axis=0, tiled=True)
    query_piece = query_wide.astype(bf16)
    gradatt_piece = gradatt_wide.astype(bf16)
    piece_docs, unused = locate(anchor_piece, lengths)
    allowed = pair_allowed(anchor_piece, piece_docs, anchor, docs)
    scores = score_scale * jnp.einsum(
        "qhd,khd->hqk", query_piece, key_rows, preferred_element_type=f32
    )
    attn_probs = jnp.where(allowed, jnp.exp(scores - logtot_piece.T[:, :, None]), 0.0)
    grad_value = jnp.einsum(
        "hqk,qhd->khd", attn_probs.astype(bf16), gradatt_piece, preferred_element_type=f32
    )
    grad_probs = jnp.einsum("qhd,khd->hqk", gradatt_piece, value_rows, preferred_element_type=f32)
    grad_scores = (attn_probs * (grad_probs - delta_piece.T[:, :, None])).astype(bf16)
    grad_key = score_scale * jnp.einsum(
        "hqk,qhd->khd", grad_scores, query_piece, preferred_element_type=f32
    )
    grad_query_hat = rotary(grad_query_rot, -positions).reshape(tok_rows, -1)
    grad_key_hat = rotary(grad_key, -positions).reshape(tok_rows, -1)
    weighted_query = grad_query_hat * query_gain
    weighted_key = grad_key_hat * key_gain
    quarter = query_gain.shape[0]
    gain_offset = lax.axis_index("tensor") * quarter
    query_gain_part = jnp.sum(grad_query_hat * query_raw * query_inv, axis=0)
    key_gain_part = jnp.sum(grad_key_hat * key_raw * key_inv, axis=0)
    query_gain_wide = lax.dynamic_update_slice_in_dim(
        jnp.zeros((D,), f32), query_gain_part, gain_offset, 0
    )
    key_gain_wide = lax.dynamic_update_slice_in_dim(
        jnp.zeros((D,), f32), key_gain_part, gain_offset, 0
    )
    cross = lax.psum(
        (
            jnp.sum(weighted_query * query_raw, axis=1),
            jnp.sum(weighted_key * key_raw, axis=1),
            query_gain_wide,
            key_gain_wide,
        ),
        "tensor",
    )
    grad_query_raw = (
        query_inv * weighted_query - query_raw * query_inv**3 * cross[0][:, None] / D
    ).astype(bf16)
    grad_key_raw = (key_inv * weighted_key - key_raw * key_inv**3 * cross[1][:, None] / D).astype(
        bf16
    )
    grad_value_low = grad_value.reshape(tok_rows, -1).astype(bf16)
    grad_query_w = contract_first(normed, grad_query_raw)
    grad_key_w = contract_first(normed, grad_key_raw)
    grad_value_w = contract_first(normed, grad_value_low)
    grad_normed = (
        contract_last(grad_query_raw, query_full)
        + contract_last(grad_key_raw, key_full)
        + contract_last(grad_value_low, value_full)
    )
    grad_normed_sum = lax.psum(grad_normed.astype(jnp.bfloat16), "tensor").astype(jnp.float32)
    grad_norm_attn, grad_attn_gain = norm_back(inputs, attn_gain, grad_normed_sum)
    input_grad = grad_resid + grad_norm_attn
    summed = (
        lax.psum_scatter(
            grad_query_w.astype(jnp.bfloat16), "dp", scatter_dimension=0, tiled=True
        ).astype(jnp.float32),
        lax.psum_scatter(
            grad_key_w.astype(jnp.bfloat16), "dp", scatter_dimension=0, tiled=True
        ).astype(jnp.float32),
        lax.psum_scatter(
            grad_value_w.astype(jnp.bfloat16), "dp", scatter_dimension=0, tiled=True
        ).astype(jnp.float32),
        lax.psum_scatter(
            grad_output_w.astype(jnp.bfloat16), "dp", scatter_dimension=0, tiled=True
        ).astype(jnp.float32),
        lax.psum_scatter(
            grad_attn_gain.astype(jnp.bfloat16), "dp", scatter_dimension=0, tiled=True
        ).astype(jnp.float32),
        lax.psum_scatter(
            cross[2].astype(jnp.bfloat16), "dp", scatter_dimension=0, tiled=True
        ).astype(jnp.float32),
        lax.psum_scatter(
            cross[3].astype(jnp.bfloat16), "dp", scatter_dimension=0, tiled=True
        ).astype(jnp.float32),
        lax.psum_scatter(
            grad_moe_gain.astype(jnp.bfloat16), "dp", scatter_dimension=0, tiled=True
        ).astype(jnp.float32),
    )
    return (
        output,
        input_grad,
        summed[0],
        summed[1],
        summed[2],
        summed[3],
        grad_gateup_w,
        grad_down,
        summed[4],
        summed[5],
        summed[6],
        summed[7],
    )


def solution(mesh):
    in_specs = (
        P("dp", None),
        P(),
        P("dp", "tensor"),
        P("dp", "tensor"),
        P("dp", "tensor"),
        P("dp", "tensor"),
        P("tensor"),
        P("tensor"),
        P(),
        P(None, "dp", None, "tensor"),
        P(None, "dp", "tensor"),
        P("dp", None),
        P("dp", None),
        P("dp"),
        P(),
        P("dp", None),
    )
    out_specs = (
        P("dp", None),
        P("dp", None),
        P("dp", "tensor"),
        P("dp", "tensor"),
        P("dp", "tensor"),
        P("dp", "tensor"),
        P(None, "dp", None, "tensor"),
        P(None, "dp", "tensor"),
        P("dp"),
        P("dp"),
        P("dp"),
        P("dp"),
    )
    return jax.shard_map(shards, mesh=mesh, in_specs=in_specs, out_specs=out_specs, check_vma=False)
```

profile of v0, /device:TPU:0, one launch (start us, length us, event | category | flops | bytes accessed | tf_op | source)
XLA Modules:
  0.0 867.9 jit_solution(12070746928078635573)
XLA Ops:
  15.4 25.0 %all-gather.10.cloned.1.call-done = bf16[2048,512]{1,0:T(8,128)(2,1)} async-done(((bf16[256,512]{1,0:T(8,128)(2,1)}), bf16[2048,512]{1,0:T(8,128)(2,1)}) %all-gather.10.cloned.1.call-update) | async-done | bytes 2097168 | tf_op jit(solution)/shard_map/all_gather | solution.py:119
  42.8 27.3 %all-gather.12.cloned.1.call-done = bf16[2048,512]{1,0:T(8,128)(2,1)} async-done(((bf16[256,512]{1,0:T(8,128)(2,1)}), bf16[2048,512]{1,0:T(8,128)(2,1)}) %all-gather.12.cloned.1.call-update) | async-done | bytes 2097168 | tf_op jit(solution)/shard_map/all_gather | solution.py:120
  72.3 11.7 %all-reduce.7 = (f32[128]{0:T(128)S(1)}, f32[128]{0:T(128)S(1)}) all-reduce(f32[128]{0:T(128)S(1)} %get-tuple-element.131, f32[128]{0:T(128)S(1)} %get-tuple-element.133), channel_id=1, replica_groups=mesh['dp'=8,'tensor'=4] {'tensor'}, use_global_device_ids=true, to_apply=%region_5.6 | all-reduce | flops 256 | bytes 2048 | tf_op jit(solution)/shard_map/psum | solution.py:127
  93.3 6.6 all-gather.16.cloned.1.call-done
  123.3 6.8 gather_fusion.2
  130.1 6.5 multiply_convert_fusion
  141.4 65.4 %all-gather = s32[8,1,128]{2,1,0:T(1,128)S(1)} all-gather(s32[1,1,128]{2,1,0:T(1,128)S(1)} %bitcast.187), channel_id=1, replica_groups=mesh['dp'=8,'tensor'=4] {'dp'}, dimensions={0}, use_global_device_ids=true | all-gather | bytes 4608 | tf_op jit(solution)/shard_map/all_gather | solution.py:143
  218.9 38.4 %all-reduce.14.cloned.1.call-done = bf16[128,2048]{1,0:T(8,128)(2,1)} async-done(((bf16[128,2048]{1,0:T(8,128)(2,1)}), bf16[128,2048]{1,0:T(8,128)(2,1)}) %all-reduce.14.cloned.1.call-update) | async-done | bytes 524304 | tf_op jit(solution)/shard_map/psum | solution.py:160
  260.4 5.9 gather_fusion
  281.0 49.4 %all-to-all-done = bf16[16,72,2048]{2,1,0:T(8,128)(2,1)} async-done(((bf16[16,72,2048]{2,1,0:T(8,128)(2,1)}), bf16[16,72,2048]{2,1,0:T(8,128)(2,1)}, u32[]{:S(2)}, u32[]{:S(2)}) %all-to-all-start) | async-done | bytes 4718624 | tf_op jit(solution)/shard_map/all_to_all | solution.py:175
  344.5 9.4 %copy.183 = bf16[2,576,2048]{2,0,1:T(2,128)(2,1)} copy(bf16[2,576,2048]{2,1,0:T(8,128)(2,1)} %bitcast_convert_fusion) | data formatting | bytes 9437184 | tf_op jit(solution)/shard_map/convert_element_type | solution.py:198
  362.5 9.3 %copy.176 = bf16[2,576,2048]{2,0,1:T(2,128)(2,1)} copy(bf16[2,576,2048]{2,1,0:T(8,128)(2,1)} %convolution_convert_fusion) | data formatting | bytes 9437184 | tf_op jit(solution)/shard_map/convert_element_type | solution.py:195
  371.8 41.7 %all-to-all-done.3 = bf16[2,576,2048]{2,0,1:T(2,128)(2,1)} async-done(((bf16[2,576,2048]{2,0,1:T(2,128)(2,1)}), bf16[2,576,2048]{2,0,1:T(2,128)(2,1)}, u32[]{:S(2)}, u32[]{:S(2)}) %all-to-all-start.3) | async-done | bytes 4718624 | tf_op jit(solution)/shard_map/all_to_all | solution.py:197
  419.4 60.7 %all_gather.49 = bf16[1024,4]{0,1:T(4,128)(2,1)S(1)} all-gather(bf16[128,4]{0,1:T(4,128)(2,1)S(1)} %copy-done.64), channel_id=1, replica_groups=mesh['dp'=8,'tensor'=4] {'dp'}, dimensions={0}, use_global_device_ids=true | all-gather | bytes 9216 | tf_op jit(solution)/shard_map/all_gather | solution.py:250
  489.5 12.6 %gather_fusion.3 = f32[1024,2048]{1,0:T(8,128)} fusion(f32[1153,2048]{1,0:T(8,128)} %pad_convert_fusion, s32[1024]{0:T(1024)S(1)} %broadcast_clamp_fusion), kind=kCustom, calls=%fused_computation.3 | custom fusion | bytes 16781312 | tf_op jit(solution)/shard_map/gather | solution.py:208
  502.1 6.2 bitcast_reduce_fusion
  511.7 6.7 copy.177
  518.5 26.7 %all-reduce.16.cloned.1.call-done = bf16[128,2048]{1,0:T(8,128)(2,1)} async-done(((bf16[128,2048]{1,0:T(8,128)(2,1)}), bf16[128,2048]{1,0:T(8,128)(2,1)}) %all-reduce.16.cloned.1.call-update) | async-done | bytes 524304 | tf_op jit(solution)/shard_map/psum | solution.py:211
  550.7 7.3 pad_convert_fusion.1
  557.9 12.6 %gather_fusion.1 = f32[1024,2048]{1,0:T(8,128)} fusion(f32[1153,2048]{1,0:T(8,128)} %pad_convert_fusion.1, s32[1024]{0:T(1024)S(1)} %broadcast_clamp_fusion), kind=kCustom, calls=%fused_computation.1 | custom fusion | bytes 16781312 | tf_op jit(solution)/shard_map/gather | solution.py:205
  570.5 7.5 fusion
  578.1 8.9 %all_gather.51 = bf16[1024,4]{0,1:T(4,128)(2,1)S(1)} all-gather(bf16[128,4]{0,1:T(4,128)(2,1)S(1)} %convert_element_type.256), channel_id=1, replica_groups=mesh['dp'=8,'tensor'=4] {'dp'}, dimensions={0}, use_global_device_ids=true | all-gather | bytes 9216 | tf_op jit(solution)/shard_map/all_gather | solution.py:253
  605.2 19.0 %all-reduce.6 = (f32[128]{0:T(128)}, f32[128]{0:T(128)S(1)}, bf16[2048]{0:T(1024)(128)(2,1)}, bf16[2048]{0:T(1024)(128)(2,1)}) all-reduce(f32[128]{0:T(128)S(1)} %get-tuple-element.79, f32[128]{0:T(128)} %get-tuple-element.77, f32[2048]{0:T(1024)S(1)} %dynamic_update_slice.6, ...), channel_id=1, replica_groups=mesh['dp'=8,'tensor'=4] {'tensor'}, use_global_device_ids=true, to_apply=%region_26.27 | all-reduce | flops 4352 | bytes 26624 | tf_op jit(solution)/shard_map/psum | solution.py:287
  645.2 8.2 convolution_bitcast_fusion
  653.4 13.3 %copy.195 = f32[2048,2,2,256]{3,2,1,0:T(2,128)} copy(f32[2048,2,2,256]{0,3,2,1:T(8,128)} %convolution_bitcast_fusion) | data formatting | bytes 16777216
  666.6 6.2 convolution_bitcast_fusion.1
  672.9 7.2 copy.196
  684.0 24.2 %all-reduce.8 = (bf16[2048]{0:T(1024)(128)(2,1)S(1)}, bf16[2048]{0:T(1024)(128)(2,1)S(1)}, bf16[2048]{0:T(1024)(128)(2,1)S(1)}, bf16[2048]{0:T(1024)(128)(2,1)S(1)}) all-reduce(bf16[2048]{0:T(1024)(128)(2,1)S(1)} %get-tuple-element.74, bf16[2048]{0:T(1024)(128)(2,1)S(1)} %copy-done.65, ...), channel_id=6, replica_groups=mesh['dp'=8,'tensor'=4] {'dp'}, use_global_device_ids=true, to_apply=%region_36.37.clone | all-reduce | flops 8192 | bytes 32768
  714.5 11.6 %reduce-scatter.11.cloned.1.call-done = bf16[256,512]{1,0:T(8,128)(2,1)} async-done(((bf16[2048,512]{1,0:T(8,128)(2,1)}), bf16[256,512]{1,0:T(8,128)(2,1)}) %reduce-scatter.11.cloned.1.call-update) | async-done | bytes 262160 | tf_op jit(solution)/shard_map/reduce_scatter | solution.py:324
  727.9 42.6 %reduce-scatter.9.cloned.1.call-done = bf16[256,512]{1,0:T(8,128)(2,1)} async-done(((bf16[2048,512]{1,0:T(8,128)(2,1)}), bf16[256,512]{1,0:T(8,128)(2,1)}) %reduce-scatter.9.cloned.1.call-update) | async-done | bytes 262160 | tf_op jit(solution)/shard_map/reduce_scatter | solution.py:321
  772.4 42.5 %reduce-scatter.7.cloned.1.call-done = bf16[256,512]{1,0:T(8,128)(2,1)} async-done(((bf16[2048,512]{1,0:T(8,128)(2,1)}), bf16[256,512]{1,0:T(8,128)(2,1)}) %reduce-scatter.7.cloned.1.call-update) | async-done | bytes 262160 | tf_op jit(solution)/shard_map/reduce_scatter | solution.py:318
  816.7 42.5 %reduce-scatter.5.cloned.1.call-done = bf16[256,512]{1,0:T(8,128)(2,1)} async-done(((bf16[2048,512]{1,0:T(8,128)(2,1)}), bf16[256,512]{1,0:T(8,128)(2,1)}) %reduce-scatter.5.cloned.1.call-update) | async-done | bytes 262160 | tf_op jit(solution)/shard_map/reduce_scatter | solution.py:315
  (337 shorter events, 181.8 us)
Async XLA Ops:
  7.2 329.5 %copy-start = (bf16[2048,2,256]{2,1,0:T(2,128)(2,1)S(1)}, bf16[2048,2,256]{2,1,0:T(2,128)(2,1)}, u32[]{:S(2)}) copy-start(bf16[2048,2,256]{2,1,0:T(2,128)(2,1)} %param.26) | copy-start | bytes 6291460
  7.2 33.2 %all-gather.10.cloned.1.call-start = ((), (), s32[]{:S(2)}) async-start(), calls=%async_computation.8 | async-start | bytes 2359296 | tf_op jit(solution)/shard_map/all_gather | solution.py:119
  7.9 62.2 %all-gather.12.cloned.1.call-start = ((), (), s32[]{:S(2)}) async-start(), calls=%async_computation.9 | async-start | bytes 2359296 | tf_op jit(solution)/shard_map/all_gather | solution.py:120
  8.7 61.4 %copy-start.2 = (bf16[128,2048]{1,0:T(8,128)(2,1)S(1)}, bf16[128,2048]{1,0:T(8,128)(2,1)}, u32[]{:S(2)}) copy-start(bf16[128,2048]{1,0:T(8,128)(2,1)} %param.16) | copy-start | bytes 1572868
  8.7 61.4 %copy-start.32 = (f32[2048]{0:T(1024)S(1)}, f32[2048]{0:T(1024)}, u32[]{:S(2)}) copy-start(f32[2048]{0:T(1024)} %param.17) | copy-start | bytes 24580
  8.7 91.1 %all-gather.16.cloned.1.call-start = ((), (), s32[]{:S(2)}) async-start(), calls=%async_computation.11 | async-start | bytes 2359296 | tf_op jit(solution)/shard_map/all_gather | solution.py:121
  9.4 198.1 %all-gather.14.cloned.1.call-start = ((), (), s32[]{:S(2)}) async-start(), calls=%async_computation.10 | async-start | bytes 1179648 | tf_op jit(solution)/shard_map/all_gather | solution.py:141
  15.4 84.4 %copy-start.53 = (f32[128]{0:T(128)}, f32[128]{0:T(128)S(1)}, u32[]{:S(2)}) copy-start(f32[128]{0:T(128)S(1)} %get-tuple-element.122) | copy-start | bytes 1540
  93.2 118.8 %all-gather.18.cloned.1.call-start = ((), (), s32[]{:S(2)}) async-start(), calls=%async_computation.12 | async-start | bytes 1179648 | tf_op jit(solution)/shard_map/all_gather | solution.py:142
  102.7 112.7 %all-gather.20.cloned.1.call-start = ((), (), s32[]{:S(2)}) async-start(), calls=%async_computation.13 | async-start | bytes 2359296 | tf_op jit(solution)/shard_map/all_gather | solution.py:122
  136.5 70.3 %copy-start.77 = (s32[4,1]{0,1:T(1,128)S(1)}, s32[4,1]{0,1:T(1,128)}, u32[]{:S(2)}) copy-start(s32[4,1]{0,1:T(1,128)} %copy-done.76) | copy-start | bytes 52
  136.5 70.4 %copy-start.71 = (s32[128]{0:T(128)S(1)}, s32[128]{0:T(128)}, u32[]{:S(2)}) copy-start(s32[128]{0:T(128)} %copy-done.70) | copy-start | bytes 1540
  136.5 70.9 %copy-start.26 = (bf16[128,4,64]{2,0,1:T(8,128)(2,1)S(1)}, bf16[128,4,64]{2,0,1:T(8,128)(2,1)}, u32[]{:S(2)}) copy-start(bf16[128,4,64]{2,0,1:T(8,128)(2,1)} %get-tuple-element.109) | copy-start | bytes 196612
  136.5 70.9 %copy-start.27 = (bf16[128,4,64]{2,0,1:T(8,128)(2,1)S(1)}, bf16[128,4,64]{2,0,1:T(8,128)(2,1)}, u32[]{:S(2)}) copy-start(bf16[128,4,64]{2,0,1:T(8,128)(2,1)} %get-tuple-element.110) | copy-start | bytes 196612
  136.6 134.6 %all-to-all-start.2 = ((bf16[16,72,2048]{2,1,0:T(8,128)(2,1)}), bf16[16,72,2048]{2,1,0:T(8,128)(2,1)}, u32[]{:S(2)}, u32[]{:S(2)}) async-start(bf16[16,72,2048]{2,1,0:T(8,128)(2,1)} %multiply_convert_fusion), calls=%async_computation.2 | async-start | bytes 9437184 | tf_op jit(solution)/shard_map/all_to_all | solution.py:176
  141.3 115.9 %all-reduce.14.cloned.1.call-start = ((), (), s32[]{:S(2)}) async-start(), calls=%async_computation.14 | async-start | bytes 1048576 | tf_op jit(solution)/shard_map/psum | solution.py:160
  271.2 59.3 %all-to-all-start = ((bf16[16,72,2048]{2,1,0:T(8,128)(2,1)}), bf16[16,72,2048]{2,1,0:T(8,128)(2,1)}, u32[]{:S(2)}, u32[]{:S(2)}) async-start(bf16[16,72,2048]{2,1,0:T(8,128)(2,1)} %broadcast_multiply_fusion), calls=%async_computation | async-start | bytes 9437184 | tf_op jit(solution)/shard_map/all_to_all | solution.py:175
  353.8 59.8 %all-to-all-start.3 = ((bf16[2,576,2048]{2,0,1:T(2,128)(2,1)}), bf16[2,576,2048]{2,0,1:T(2,128)(2,1)}, u32[]{:S(2)}, u32[]{:S(2)}) async-start(bf16[2,576,2048]{2,0,1:T(2,128)(2,1)} %copy.183), calls=%async_computation.3 | async-start | bytes 9437184 | tf_op jit(solution)/shard_map/all_to_all | solution.py:197
  371.8 47.2 %copy-start.40 = (s32[1024]{0:T(1024)S(1)}, s32[1024]{0:T(1024)}, u32[]{:S(2)}) copy-start(s32[1024]{0:T(1024)} %copy-done.39) | copy-start | bytes 12292
  371.8 47.3 %copy-start.61 = (s32[128]{0:T(128)S(1)}, s32[128]{0:T(128)}, u32[]{:S(2)}) copy-start(s32[128]{0:T(128)} %param.29) | copy-start | bytes 1540
  371.8 47.3 %copy-start.72 = (s32[128]{0:T(128)S(1)}, s32[128]{0:T(128)}, u32[]{:S(2)}) copy-start(s32[128]{0:T(128)} %copy-done.70) | copy-start | bytes 1540
  371.8 47.6 %copy-start.64 = (bf16[128,4]{0,1:T(4,128)(2,1)S(1)}, bf16[128,4]{0,1:T(4,128)(2,1)}, u32[]{:S(2)}) copy-start(bf16[128,4]{0,1:T(4,128)(2,1)} %get-tuple-element.113) | copy-start | bytes 3076
  413.6 98.2 %all-to-all-start.1 = ((bf16[2,576,2048]{2,0,1:T(2,128)(2,1)}), bf16[2,576,2048]{2,0,1:T(2,128)(2,1)}, u32[]{:S(2)}, u32[]{:S(2)}) async-start(bf16[2,576,2048]{2,0,1:T(2,128)(2,1)} %copy.176), calls=%async_computation.1 | async-start | bytes 9437184 | tf_op jit(solution)/shard_map/all_to_all | solution.py:194
  418.2 90.2 %all-gather.22.cloned.1.call-start = ((), (), s32[]{:S(2)}) async-start(), calls=%async_computation.16 | async-start | bytes 1179648 | tf_op jit(solution)/shard_map/all_gather | solution.py:244
  419.0 126.2 %all-reduce.16.cloned.1.call-start = ((), (), s32[]{:S(2)}) async-start(), calls=%async_computation.15 | async-start | bytes 1048576 | tf_op jit(solution)/shard_map/psum | solution.py:211
  508.3 82.3 %all-gather.24.cloned.1.call-start = ((), (), s32[]{:S(2)}) async-start(), calls=%async_computation.17 | async-start | bytes 1179648 | tf_op jit(solution)/shard_map/all_gather | solution.py:247
  550.4 132.2 %all-reduce.18.cloned.1.call-start = ((), (), s32[]{:S(2)}) async-start(), calls=%async_computation.22 | async-start | bytes 2097152 | tf_op jit(solution)/shard_map/psum | solution.py:210
  633.2 92.9 %reduce-scatter.11.cloned.1.call-start = ((), (), s32[]{:S(2)}) async-start(), calls=%async_computation.21 | async-start | bytes 2359296 | tf_op jit(solution)/shard_map/reduce_scatter | solution.py:324
  636.5 134.1 %reduce-scatter.9.cloned.1.call-start = ((), (), s32[]{:S(2)}) async-start(), calls=%async_computation.20 | async-start | bytes 2359296 | tf_op jit(solution)/shard_map/reduce_scatter | solution.py:321
  639.4 175.5 %reduce-scatter.7.cloned.1.call-start = ((), (), s32[]{:S(2)}) async-start(), calls=%async_computation.19 | async-start | bytes 2359296 | tf_op jit(solution)/shard_map/reduce_scatter | solution.py:318
  641.7 217.5 %reduce-scatter.5.cloned.1.call-start = ((), (), s32[]{:S(2)}) async-start(), calls=%async_computation.18 | async-start | bytes 2359296 | tf_op jit(solution)/shard_map/reduce_scatter | solution.py:315
  710.8 150.1 %copy-start.1 = (bf16[2048,2,256]{2,1,0:T(2,128)(2,1)S(1)}, bf16[2048,2,256]{2,1,0:T(2,128)(2,1)}, u32[]{:S(2)}) copy-start(bf16[2048,2,256]{2,1,0:T(2,128)(2,1)} %param.26) | copy-start | bytes 6291460
  (73 other events, 1012.0 us)
Sparse Core Ops, SparseCore 0:
  9.9 30.4 all-gather.9
  42.3 27.7 all-gather.11
  72.0 27.7 all-gather.15
  102.2 23.3 all-gather.13
  127.9 26.3 all-gather.17
  156.0 52.6 all-gather.19
  218.9 38.3 all-reduce.13
  420.9 35.1 all-gather.21
  508.5 36.7 all-reduce.15
  550.5 23.2 all-gather.23
  633.3 49.2 all-reduce.17
  685.8 40.3 reduce-scatter.10
  729.4 41.1 reduce-scatter.8
  773.7 41.1 reduce-scatter.6
  818.0 41.1 reduce-scatter.4
where the time goes:
time: 877 us; the launch traced here: 868 us
  waiting for transfers between devices  360 us (41%)
  blocking collectives  190 us (22%)
  local copies, waits for them, and re-layouts  129 us (15%)
  other arithmetic  83.5 us (10%)
  matrix products  69.1 us (8%)
  starting transfers between devices  20.1 us (2%)
  between operations  16.2 us (2%)
    all_gather x1, blocking collectives, shards(): anchor_piece = lax.all_gather(anchor, 'dp', axis=0, tiled=True)  65.4 us
    all_gather x1, blocking collectives, shards(): lax.all_gather(log_total.T.astype(jnp.bfloat16), 'dp', axis=0, tiled=True)  60.7 us
    all_to_all x1, waiting for transfers between devices, shards(): lax.all_to_all(buffer_rows, 'dp', split_axis=0, concat_axis=1, tiled=True)  49.4 us
    reduce_scatter x1, waiting for transfers between devices, shards(): lax.psum_scatter(grad_value_w.astype(jnp.bfloat16), 'dp', scatter_dimensi...  42.6 us
    reduce_scatter x1, waiting for transfers between devices, shards(): lax.psum_scatter(grad_key_w.astype(jnp.bfloat16), 'dp', scatter_dimension...  42.5 us
    reduce_scatter x1, waiting for transfers between devices, shards(): lax.psum_scatter(grad_query_w.astype(jnp.bfloat16), 'dp', scatter_dimensi...  42.5 us
    all_to_all x1, waiting for transfers between devices, shards(): lax.all_to_all(grad_buffer.astype(jnp.bfloat16), 'dp', split_axis=1, conc...  41.7 us
    psum x1, waiting for transfers between devices, shards(): lax.psum(contract_last(attended_low, output_full).astype(jnp.bfloat16), '...  38.4 us
  transfers between devices with their start and end apart: 19, of which 12 were waited for; matrix products, arithmetic and copies ran while one was open for 26% of the time, Pallas kernels for 0%

commit v1 on v0

--- a/solution.py
+++ b/solution.py
@@ -9,6 +9,19 @@
 EPSILON = 1e-05
 ROPE_BASE = 10000.0
 NEG_FILL = -1e30
+
+
+def gather_around(x, axis, dim):
+    ways = lax.axis_size(axis)
+    up = [(d, (d + 1) % ways) for d in range(ways)]
+    down = [(d, (d - 1) % ways) for d in range(ways)]
+    earlier, later = ([x], [x])
+    for _ in range(ways // 2):
+        earlier.append(lax.ppermute(earlier[-1], axis, up))
+    for _ in range((ways - 1) // 2):
+        later.append(lax.ppermute(later[-1], axis, down))
+    line = jnp.concatenate([*earlier[::-1], *later[1:]], axis=dim)
+    return jnp.roll(line, (lax.axis_index(axis) - ways // 2) * x.shape[dim], axis=dim)
 
 
 def rms_norm(values, gain):
@@ -117,7 +130,7 @@
     normed = rms_norm(inputs, attn_gain).astype(bf16)
     query_full, key_full, value_full, output_full = (
         lax.all_gather(query_weight, "dp", axis=0, tiled=True),
-        lax.all_gather(key_weight, "dp", axis=0, tiled=True),
+        gather_around(key_weight, "dp", 0),
         lax.all_gather(value_weight, "dp", axis=0, tiled=True),
         lax.all_gather(output_weight, "dp", axis=0, tiled=True),
     )

time: 877 us -> 837 us (0.954)
  waiting for transfers between devices: 360 us -> 311 us
  blocking collectives: 190 us -> 173 us
  starting transfers between devices: 20.1 us -> 32.9 us
  matrix products: 69.1 us -> 78.7 us
    all_gather x1, waiting for transfers between devices: 27.3 us -> 0.01 us  [shards(): lax.all_gather(key_weight, 'dp', axis=0, tiled=True)]
    all_gather x1, waiting for transfers between devices: 25 us -> 0.02 us  [shards(): lax.all_gather(query_weight, 'dp', axis=0, tiled=True)]
    all_gather x1, blocking collectives: 60.7 us -> 36.2 us  [shards(): lax.all_gather(log_total.T.astype(jnp.bfloat16), 'dp', axis=0, tiled=True)]
    ppermute x0 -> x7, waiting for transfers between devices: none -> 13.2 us  [the longest x4 13.2 us: gather_around(): earlier.append(lax.ppermute(earlier[-1], axis, up))]
    all_to_all x1, waiting for transfers between devices: 41.7 us -> 54.2 us  [shards(): lax.all_to_all(grad_buffer.astype(jnp.bfloat16), 'dp', split_axis=1, conc...]
    ppermute x0 -> x7, starting transfers between devices: none -> 12 us  [the longest x4 8.91 us: gather_around(): earlier.append(lax.ppermute(earlier[-1], axis, up))]
    psum x1, waiting for transfers between devices: 26.7 us -> 17.1 us  [shards(): lax.psum(grad_moe_part.astype(jnp.bfloat16), 'tensor').astype(jnp.float32)]
    unnamed x177 -> x134, local copies, waits for them, and re-layouts: 28.1 us -> 33.4 us
  transfers between devices with their start and end apart: 19 -> 26, of which waited for: 12 -> 12; matrix products, arithmetic and copies ran while one was open for 26% -> 28% of each run, Pallas kernels for 0% -> 0%
where the time goes in v1:
time: 837 us; the launch traced here: 827 us
  waiting for transfers between devices  311 us (37%)
  blocking collectives  173 us (21%)
  local copies, waits for them, and re-layouts  132 us (16%)
  other arithmetic  82.3 us (10%)
  matrix products  78.7 us (9%)
  starting transfers between devices  32.9 us (4%)
  between operations  16.1 us (2%)
    all_gather x1, blocking collectives, shards(): anchor_piece = lax.all_gather(anchor, 'dp', axis=0, tiled=True)  67.7 us
    all_to_all x1, waiting for transfers between devices, shards(): lax.all_to_all(grad_buffer.astype(jnp.bfloat16), 'dp', split_axis=1, conc...  54.2 us
    all_to_all x1, waiting for transfers between devices, shards(): lax.all_to_all(buffer_rows, 'dp', split_axis=0, concat_axis=1, tiled=True)  49.4 us
    reduce_scatter x1, waiting for transfers between devices, shards(): lax.psum_scatter(grad_value_w.astype(jnp.bfloat16), 'dp', scatter_dimensi...  42.6 us
    reduce_scatter x1, waiting for transfers between devices, shards(): lax.psum_scatter(grad_query_w.astype(jnp.bfloat16), 'dp', scatter_dimensi...  42.5 us
    reduce_scatter x1, waiting for transfers between devices, shards(): lax.psum_scatter(grad_key_w.astype(jnp.bfloat16), 'dp', scatter_dimension...  42.5 us
    all_gather x1, blocking collectives, shards(): lax.all_gather(log_total.T.astype(jnp.bfloat16), 'dp', axis=0, tiled=True)  36.2 us
    psum x1, waiting for transfers between devices, shards(): lax.psum(contract_last(attended_low, output_full).astype(jnp.bfloat16), '...  35.5 us
  transfers between devices with their start and end apart: 26, of which 12 were waited for; matrix products, arithmetic and copies ran while one was open for 28% of the time, Pallas kernels for 0%

profile of v1, /device:TPU:0, one launch (start us, length us, event | category | flops | bytes accessed | tf_op | source)
XLA Modules:
  0.0 827.0 jit_solution(9569353878511323499)
XLA Ops:
  17.3 5.3 collective-permute-done.1
  29.4 5.2 collective-permute-start.3
  50.3 18.7 %all-reduce.7 = (f32[128]{0:T(128)S(1)}, f32[128]{0:T(128)S(1)}) all-reduce(f32[128]{0:T(128)S(1)} %get-tuple-element.131, f32[128]{0:T(128)S(1)} %get-tuple-element.133), channel_id=1, replica_groups=mesh['dp'=8,'tensor'=4] {'tensor'}, use_global_device_ids=true, to_apply=%region_5.6 | all-reduce | flops 256 | bytes 2048 | tf_op jit(solution)/shard_map/psum | solution.py:140
  101.8 6.9 gather_fusion.2
  108.6 6.6 multiply_convert_fusion
  115.2 5.5 all-to-all-start.2
  120.7 67.7 %all-gather = s32[8,1,128]{2,1,0:T(1,128)S(1)} all-gather(s32[1,1,128]{2,1,0:T(1,128)S(1)} %bitcast.186), channel_id=1, replica_groups=mesh['dp'=8,'tensor'=4] {'dp'}, dimensions={0}, use_global_device_ids=true | all-gather | bytes 4608 | tf_op jit(solution)/shard_map/all_gather | solution.py:156
  199.6 35.5 %all-reduce.14.cloned.1.call-done = bf16[128,2048]{1,0:T(8,128)(2,1)} async-done(((bf16[128,2048]{1,0:T(8,128)(2,1)}), bf16[128,2048]{1,0:T(8,128)(2,1)}) %all-reduce.14.cloned.1.call-update) | async-done | bytes 524304 | tf_op jit(solution)/shard_map/psum | solution.py:173
  237.7 5.9 gather_fusion
  253.2 5.3 copy.180
  258.5 49.4 %all-to-all-done = bf16[16,72,2048]{2,1,0:T(8,128)(2,1)} async-done(((bf16[16,72,2048]{2,1,0:T(8,128)(2,1)}), bf16[16,72,2048]{2,1,0:T(8,128)(2,1)}, u32[]{:S(2)}, u32[]{:S(2)}) %all-to-all-start) | async-done | bytes 4718624 | tf_op jit(solution)/shard_map/all_to_all | solution.py:188
  322.7 9.4 %copy.183 = bf16[2,576,2048]{2,0,1:T(2,128)(2,1)} copy(bf16[2,576,2048]{2,1,0:T(8,128)(2,1)} %bitcast_convert_fusion) | data formatting | bytes 9437184 | tf_op jit(solution)/shard_map/convert_element_type | solution.py:211
  337.2 54.2 %all-to-all-done.3 = bf16[2,576,2048]{2,0,1:T(2,128)(2,1)} async-done(((bf16[2,576,2048]{2,0,1:T(2,128)(2,1)}), bf16[2,576,2048]{2,0,1:T(2,128)(2,1)}, u32[]{:S(2)}, u32[]{:S(2)}) %all-to-all-start.3) | async-done | bytes 4718624 | tf_op jit(solution)/shard_map/all_to_all | solution.py:210
  400.8 12.6 %gather_fusion.3 = f32[1024,2048]{1,0:T(8,128)} fusion(f32[1153,2048]{1,0:T(8,128)} %pad_convert_fusion, s32[1024]{0:T(1024)S(1)} %broadcast_clamp_fusion), kind=kCustom, calls=%fused_computation.3 | custom fusion | bytes 16781312 | tf_op jit(solution)/shard_map/gather | solution.py:221
  413.4 6.2 bitcast_reduce_fusion
  425.0 9.4 %copy.176 = bf16[2,576,2048]{2,0,1:T(2,128)(2,1)} copy(bf16[2,576,2048]{2,1,0:T(8,128)(2,1)} %convolution_convert_fusion) | data formatting | bytes 9437184 | tf_op jit(solution)/shard_map/convert_element_type | solution.py:208
  439.2 17.1 %all-reduce.16.cloned.1.call-done = bf16[128,2048]{1,0:T(8,128)(2,1)} async-done(((bf16[128,2048]{1,0:T(8,128)(2,1)}), bf16[128,2048]{1,0:T(8,128)(2,1)}) %all-reduce.16.cloned.1.call-update) | async-done | bytes 524304 | tf_op jit(solution)/shard_map/psum | solution.py:224
  464.8 36.2 %all_gather.47 = bf16[1024,4]{0,1:T(4,128)(2,1)S(1)} all-gather(bf16[128,4]{0,1:T(4,128)(2,1)S(1)} %get-tuple-element.113), channel_id=1, replica_groups=mesh['dp'=8,'tensor'=4] {'dp'}, dimensions={0}, use_global_device_ids=true | all-gather | bytes 9216 | tf_op jit(solution)/shard_map/all_gather | solution.py:263
  509.5 4.9 pad_convert_fusion.1
  514.5 12.7 %gather_fusion.1 = f32[1024,2048]{1,0:T(8,128)} fusion(f32[1153,2048]{1,0:T(8,128)} %pad_convert_fusion.1, s32[1024]{0:T(1024)S(1)} %broadcast_clamp_fusion), kind=kCustom, calls=%fused_computation.1 | custom fusion | bytes 16781312 | tf_op jit(solution)/shard_map/gather | solution.py:218
  527.2 7.4 fusion
  534.7 8.2 all_gather.49
  562.7 18.4 %all-reduce.6 = (f32[128]{0:T(128)}, f32[128]{0:T(128)}, bf16[2048]{0:T(1024)(128)(2,1)}, bf16[2048]{0:T(1024)(128)(2,1)}) all-reduce(f32[128]{0:T(128)S(1)} %get-tuple-element.79, f32[128]{0:T(128)S(1)} %get-tuple-element.77, f32[2048]{0:T(1024)S(1)} %dynamic_update_slice.6, ...), channel_id=1, replica_groups=mesh['dp'=8,'tensor'=4] {'tensor'}, use_global_device_ids=true, to_apply=%region_26.27 | all-reduce | flops 4352 | bytes 26624 | tf_op jit(solution)/shard_map/psum | solution.py:300
  605.5 9.5 %convolution_bitcast_fusion = f32[2048,2,2,256]{0,3,2,1:T(8,128)} fusion(bf16[2,576,2048,1]{2,1,3,0:T(8,128)(2,1)} %bitcast.163, bf16[2,576,1,256]{3,1,0,2:T(8,128)(2,1)} %copy-done.54, bf16[2,576,1,256]{3,1,0,2:T(8,128)(2,1)} %copy-done.53), kind=kOutput, calls=%fused_computation.14 | convolution fusion | flops 2416508928 | bytes 14286848 | tf_op jit(solution)/shard_map/ecd,eczf->dezf/dot_general | solution.py:202
  615.0 13.2 %copy.195 = f32[2048,2,2,256]{3,2,1,0:T(2,128)} copy(f32[2048,2,2,256]{0,3,2,1:T(8,128)} %convolution_bitcast_fusion) | data formatting | bytes 16777216
  628.2 6.3 convolution_bitcast_fusion.1
  634.5 7.2 copy.196
  643.2 24.1 %all-reduce.8 = (bf16[2048]{0:T(1024)(128)(2,1)S(1)}, bf16[2048]{0:T(1024)(128)(2,1)S(1)}, bf16[2048]{0:T(1024)(128)(2,1)S(1)}, bf16[2048]{0:T(1024)(128)(2,1)S(1)}) all-reduce(bf16[2048]{0:T(1024)(128)(2,1)S(1)} %get-tuple-element.74, bf16[2048]{0:T(1024)(128)(2,1)S(1)} %copy-done.40, ...), channel_id=6, replica_groups=mesh['dp'=8,'tensor'=4] {'dp'}, use_global_device_ids=true, to_apply=%region_36.37.clone | all-reduce | flops 8192 | bytes 32768
  673.4 11.8 %reduce-scatter.11.cloned.1.call-done = bf16[256,512]{1,0:T(8,128)(2,1)} async-done(((bf16[2048,512]{1,0:T(8,128)(2,1)}), bf16[256,512]{1,0:T(8,128)(2,1)}) %reduce-scatter.11.cloned.1.call-update) | async-done | bytes 262160 | tf_op jit(solution)/shard_map/reduce_scatter | solution.py:337
  687.0 42.6 %reduce-scatter.9.cloned.1.call-done = bf16[256,512]{1,0:T(8,128)(2,1)} async-done(((bf16[2048,512]{1,0:T(8,128)(2,1)}), bf16[256,512]{1,0:T(8,128)(2,1)}) %reduce-scatter.9.cloned.1.call-update) | async-done | bytes 262160 | tf_op jit(solution)/shard_map/reduce_scatter | solution.py:334
  731.4 42.5 %reduce-scatter.7.cloned.1.call-done = bf16[256,512]{1,0:T(8,128)(2,1)} async-done(((bf16[2048,512]{1,0:T(8,128)(2,1)}), bf16[256,512]{1,0:T(8,128)(2,1)}) %reduce-scatter.7.cloned.1.call-update) | async-done | bytes 262160 | tf_op jit(solution)/shard_map/reduce_scatter | solution.py:331
  775.7 42.5 %reduce-scatter.5.cloned.1.call-done = bf16[256,512]{1,0:T(8,128)(2,1)} async-done(((bf16[2048,512]{1,0:T(8,128)(2,1)}), bf16[256,512]{1,0:T(8,128)(2,1)}) %reduce-scatter.5.cloned.1.call-update) | async-done | bytes 262160 | tf_op jit(solution)/shard_map/reduce_scatter | solution.py:328
  (309 shorter events, 202.6 us)
Async XLA Ops:
  7.2 307.0 %copy-start = (bf16[2048,2,256]{2,1,0:T(2,128)(2,1)S(1)}, bf16[2048,2,256]{2,1,0:T(2,128)(2,1)}, u32[]{:S(2)}) copy-start(bf16[2048,2,256]{2,1,0:T(2,128)(2,1)} %param.26) | copy-start | bytes 6291460
  7.2 40.8 %all-gather.10.cloned.1.call-start = ((), (), s32[]{:S(2)}) async-start(), calls=%async_computation.8 | async-start | bytes 2359296 | tf_op jit(solution)/shard_map/all_gather | solution.py:132
  7.9 70.3 %all-gather.14.cloned.1.call-start = ((), (), s32[]{:S(2)}) async-start(), calls=%async_computation.10 | async-start | bytes 2359296 | tf_op jit(solution)/shard_map/all_gather | solution.py:134
  8.0 7.9 collective-permute-start
  8.5 17.6 %collective-permute-start.4 = (bf16[256,512]{1,0:T(8,128)(2,1)}, bf16[256,512]{1,0:T(8,128)(2,1)S(1)}, u32[]{:S(2)}, u32[]{:S(2)}) collective-permute-start(bf16[256,512]{1,0:T(8,128)(2,1)} %param.19), channel_id=1, source_target_pairs={{0,28},{4,0},{8,4},{12,8},{16,12},{20,16},{24,20},{28,24},{1,29},{... | collective-permute-start | bytes 786440 | tf_op jit(solution)/shard_map/ppermute | solution.py:22
  11.5 177.4 %all-gather.12.cloned.1.call-start = ((), (), s32[]{:S(2)}) async-start(), calls=%async_computation.9 | async-start | bytes 1179648 | tf_op jit(solution)/shard_map/all_gather | solution.py:154
  15.9 6.7 collective-permute-start.1
  22.6 6.8 collective-permute-start.2
  26.1 10.6 %collective-permute-start.5 = (bf16[256,512]{1,0:T(8,128)(2,1)S(1)}, bf16[256,512]{1,0:T(8,128)(2,1)}, u32[]{:S(2)}, u32[]{:S(2)}) collective-permute-start(bf16[256,512]{1,0:T(8,128)(2,1)S(1)} %collective-permute-done.4), channel_id=1, source_target_pairs={{0,28},{4,0},{8,4},{12,8},{16,12},{20,16},{24,20},{28,24},{1,29},{... | collective-permute-start | bytes 786440 | tf_op jit(solution)/shard_map/ppermute | solution.py:22
  29.4 9.9 %collective-permute-start.3 = (bf16[256,512]{1,0:T(8,128)(2,1)}, bf16[256,512]{1,0:T(8,128)(2,1)}, u32[]{:S(2)}, u32[]{:S(2)}) collective-permute-start(bf16[256,512]{1,0:T(8,128)(2,1)} %collective-permute-done.2), channel_id=1, source_target_pairs={{0,4},{4,8},{8,12},{12,16},{16,20},{20,24},{24,28},{28,0},{1,5},{5... | collective-permute-start | bytes 786440 | tf_op jit(solution)/shard_map/ppermute | solution.py:20
  36.6 7.6 collective-permute-start.6
  78.2 114.6 %all-gather.16.cloned.1.call-start = ((), (), s32[]{:S(2)}) async-start(), calls=%async_computation.11 | async-start | bytes 1179648 | tf_op jit(solution)/shard_map/all_gather | solution.py:155
  81.2 115.0 %all-gather.18.cloned.1.call-start = ((), (), s32[]{:S(2)}) async-start(), calls=%async_computation.12 | async-start | bytes 2359296 | tf_op jit(solution)/shard_map/all_gather | solution.py:135
  115.2 73.4 %copy-start.43 = (s32[128]{0:T(128)S(1)}, s32[128]{0:T(128)}, u32[]{:S(2)}) copy-start(s32[128]{0:T(128)} %copy-done.42) | copy-start | bytes 1540
  115.2 73.6 %copy-start.18 = (bf16[128,4,64]{2,0,1:T(8,128)(2,1)S(1)}, bf16[128,4,64]{2,0,1:T(8,128)(2,1)}, u32[]{:S(2)}) copy-start(bf16[128,4,64]{2,0,1:T(8,128)(2,1)} %get-tuple-element.109) | copy-start | bytes 196612
  115.2 73.6 %copy-start.19 = (bf16[128,4,64]{2,0,1:T(8,128)(2,1)S(1)}, bf16[128,4,64]{2,0,1:T(8,128)(2,1)}, u32[]{:S(2)}) copy-start(bf16[128,4,64]{2,0,1:T(8,128)(2,1)} %get-tuple-element.110) | copy-start | bytes 196612
  115.2 133.4 %all-to-all-start.2 = ((bf16[16,72,2048]{2,1,0:T(8,128)(2,1)}), bf16[16,72,2048]{2,1,0:T(8,128)(2,1)}, u32[]{:S(2)}, u32[]{:S(2)}) async-start(bf16[16,72,2048]{2,1,0:T(8,128)(2,1)} %multiply_convert_fusion), calls=%async_computation.2 | async-start | bytes 9437184 | tf_op jit(solution)/shard_map/all_to_all | solution.py:189
  120.7 114.5 %all-reduce.14.cloned.1.call-start = ((), (), s32[]{:S(2)}) async-start(), calls=%async_computation.13 | async-start | bytes 1048576 | tf_op jit(solution)/shard_map/psum | solution.py:173
  236.4 221.8 %copy-start.34 = (f32[128]{0:T(128)}, f32[128]{0:T(128)S(1)}, u32[]{:S(2)}) copy-start(f32[128]{0:T(128)S(1)} %get-tuple-element.130) | copy-start | bytes 1540
  236.5 221.8 %copy-start.44 = (f32[128]{0:T(128)}, f32[128]{0:T(128)S(1)}, u32[]{:S(2)}) copy-start(f32[128]{0:T(128)S(1)} %get-tuple-element.129) | copy-start | bytes 1540
  248.6 59.4 %all-to-all-start = ((bf16[16,72,2048]{2,1,0:T(8,128)(2,1)}), bf16[16,72,2048]{2,1,0:T(8,128)(2,1)}, u32[]{:S(2)}, u32[]{:S(2)}) async-start(bf16[16,72,2048]{2,1,0:T(8,128)(2,1)} %broadcast_multiply_fusion), calls=%async_computation | async-start | bytes 9437184 | tf_op jit(solution)/shard_map/all_to_all | solution.py:188
  332.1 59.3 %all-to-all-start.3 = ((bf16[2,576,2048]{2,0,1:T(2,128)(2,1)}), bf16[2,576,2048]{2,0,1:T(2,128)(2,1)}, u32[]{:S(2)}, u32[]{:S(2)}) async-start(bf16[2,576,2048]{2,0,1:T(2,128)(2,1)} %copy.183), calls=%async_computation.3 | async-start | bytes 9437184 | tf_op jit(solution)/shard_map/all_to_all | solution.py:210
  336.7 119.6 %all-reduce.16.cloned.1.call-start = ((), (), s32[]{:S(2)}) async-start(), calls=%async_computation.14 | async-start | bytes 1048576 | tf_op jit(solution)/shard_map/psum | solution.py:224
  419.6 82.1 %all-gather.20.cloned.1.call-start = ((), (), s32[]{:S(2)}) async-start(), calls=%async_computation.15 | async-start | bytes 1179648 | tf_op jit(solution)/shard_map/all_gather | solution.py:257
  434.4 70.6 %all-to-all-start.1 = ((bf16[2,576,2048]{2,0,1:T(2,128)(2,1)}), bf16[2,576,2048]{2,0,1:T(2,128)(2,1)}, u32[]{:S(2)}, u32[]{:S(2)}) async-start(bf16[2,576,2048]{2,0,1:T(2,128)(2,1)} %copy.176), calls=%async_computation.1 | async-start | bytes 9437184 | tf_op jit(solution)/shard_map/all_to_all | solution.py:207
  439.1 108.6 %all-gather.22.cloned.1.call-start = ((), (), s32[]{:S(2)}) async-start(), calls=%async_computation.16 | async-start | bytes 1179648 | tf_op jit(solution)/shard_map/all_gather | solution.py:260
  463.1 124.5 %all-gather.24.cloned.1.call-start = ((), (), s32[]{:S(2)}) async-start(), calls=%async_computation.17 | async-start | bytes 2359296 | tf_op jit(solution)/shard_map/all_gather | solution.py:229
  463.7 178.0 %all-reduce.18.cloned.1.call-start = ((), (), s32[]{:S(2)}) async-start(), calls=%async_computation.22 | async-start | bytes 2097152 | tf_op jit(solution)/shard_map/psum | solution.py:223
  592.2 93.0 %reduce-scatter.11.cloned.1.call-start = ((), (), s32[]{:S(2)}) async-start(), calls=%async_computation.21 | async-start | bytes 2359296 | tf_op jit(solution)/shard_map/reduce_scatter | solution.py:337
  595.8 133.8 %reduce-scatter.9.cloned.1.call-start = ((), (), s32[]{:S(2)}) async-start(), calls=%async_computation.20 | async-start | bytes 2359296 | tf_op jit(solution)/shard_map/reduce_scatter | solution.py:334
  598.7 175.2 %reduce-scatter.7.cloned.1.call-start = ((), (), s32[]{:S(2)}) async-start(), calls=%async_computation.19 | async-start | bytes 2359296 | tf_op jit(solution)/shard_map/reduce_scatter | solution.py:331
  601.6 216.5 %reduce-scatter.5.cloned.1.call-start = ((), (), s32[]{:S(2)}) async-start(), calls=%async_computation.18 | async-start | bytes 2359296 | tf_op jit(solution)/shard_map/reduce_scatter | solution.py:328
  (51 other events, 836.1 us)
Sparse Core Ops, SparseCore 0:
  9.9 34.4 all-gather.9
  46.2 30.1 all-gather.13
  78.9 23.3 all-gather.11
  104.6 26.1 all-gather.15
  132.5 55.3 all-gather.17
  199.6 35.4 all-reduce.13
  419.7 36.5 all-reduce.15
  458.2 39.5 all-gather.19
  499.6 22.5 all-gather.21
  523.9 27.7 all-gather.23
  592.3 49.3 all-reduce.17
  644.8 40.3 reduce-scatter.10
  688.4 41.1 reduce-scatter.8
  732.7 41.0 reduce-scatter.6
  777.0 41.1 reduce-scatter.4
